TPU v7x, 32 devices: a 4x4x1 block of a 4x4x8 slice. The times are simulated.
32 devices in a mesh: dp: 1 (over z), vp: 32 (over y, x, core).
Axes of the slice: x: 4, y: 4, z: 1, core: 2. Of those that a mesh axis runs over, the one named last changes fastest.
The devices are a block of a 4x4x8 slice.
Arguments:
- hidden: bfloat16 [1024, 4096], P('dp')
- w_head: bfloat16 [4096, 128256], P(None, 'vp')
- inv_temp: float32 [1024], P('dp')
- target: int32 [1024], P('dp')
Outputs:
- output 1: float32 [1024, 128256], P('dp', 'vp')
- output 2: float32 [1024], P('dp')
All inputs are finite; a program needn't handle non-finite values.
Results may differ from a plain program's by a relative error of at most 0.001.
Values are sent between devices in bfloat16 or wider.
A program may use at most 768 MiB of HBM per device.

v0:
```python
import jax
import jax.numpy as jnp
from jax import lax
from jax.sharding import PartitionSpec as P, NamedSharding


def solution(mesh):
    def local_fn(h_rows, w_cols, tau_rows, tgt_rows):
        shard_width = w_cols.shape[1]
        shard_idx = lax.axis_index("vp")
        logits = jnp.dot(h_rows, w_cols, preferred_element_type=jnp.float32) * tau_rows[:, None]
        local_max = jnp.max(logits, axis=1)
        run_sum = jnp.cumsum(jnp.exp(logits - local_max[:, None]), axis=1)
        pair_stats = jnp.stack([local_max, run_sum[:, -1]])
        all_stats = lax.all_gather(pair_stats, "vp")
        all_maxes = all_stats[:, 0]
        all_sums = all_stats[:, 1]
        glob_max = jnp.max(all_maxes, axis=0)
        scaled = all_sums * jnp.exp(all_maxes - glob_max[None, :])
        glob_sum = jnp.sum(scaled, axis=0)
        before = (jnp.arange(all_stats.shape[0]) < shard_idx)[:, None]
        offset = jnp.sum(jnp.where(before, scaled, 0.0), axis=0)
        cdf_local = (run_sum * jnp.exp(local_max - glob_max)[:, None] + offset[:, None]) / glob_sum[:, None]
        local_pos = tgt_rows - shard_idx * shard_width
        inside = (local_pos >= 0) & (local_pos < shard_width)
        picked = jnp.take_along_axis(cdf_local, jnp.clip(local_pos, 0, shard_width - 1)[:, None], axis=1)[:, 0]
        cdf_target = lax.psum(jnp.where(inside, picked, 0.0), "vp")
        return cdf_local, cdf_target

    return jax.shard_map(
        local_fn,
        mesh=mesh,
        in_specs=(P("dp", None), P(None, "vp"), P("dp"), P("dp")),
        out_specs=(P("dp", "vp"), P("dp")),
        check_vma=False,
    )
```

profile of v0, /device:TPU:97, one launch (start us, length us, event | category | flops | bytes accessed | tf_op | source)
XLA Modules:
  0.0 239.3 jit_solution(13436937675011585117)
XLA Ops:
  0.6 0.0 copy-start.2
  0.6 42.8 %multiply_reduce_fusion = (f32[1024]{0:T(1024)S(1)}, f32[1024,4008]{0,1:T(8,128)S(1)}) fusion(f32[1024]{0:T(1024)} %param.6, bf16[1024,4096]{1,0:T(8,128)(2,1)} %param.4, bf16[4096,4008]{0,1:T(8,128)(2,1)} %param.5), kind=kOutput, calls=%fused_computation.7 | convolution fusion | flops 33629749248 | bytes 57647104 | tf_op jit(solution)/shard_map/dot_general | solution.py:11
  43.5 0.0 copy-done.2
  43.5 2.3 subtract_exponential_fusion
  45.8 7.2 %pad.3 = f32[1024,4096]{0,1:T(8,128)} pad(f32[1024,4008]{0,1:T(8,128)S(1)} %subtract_exponential_fusion, f32[]{:T(128)} %constant.11.clone.1), padding=0_0x0_88 | pad | bytes 33193988 | tf_op jit(solution)/shard_map/pad
  53.0 19.5 %fusion = f32[1024,32,128]{0,1,2:T(8,128)} fusion(f32[1024,32,128]{0,2,1:T(8,128)} %bitcast.34), kind=kOutput, calls=%fused_computation.1 | output fusion | flops 532676608 | bytes 33554432 | tf_op jit(solution)/shard_map/reduce-window
  72.5 0.9 slice_bitcast_fusion
  73.4 0.1 reduce-window.9
  73.6 6.8 %broadcast_add_fusion = f32[1024,32,128]{0,1,2:T(8,128)S(1)} fusion(f32[1024,32,128]{0,1,2:T(8,128)} %fusion, f32[1024,32]{0,1:T(8,128)S(1)} %slice.28), kind=kLoop, calls=%fused_computation.8 | loop fusion | flops 4194304 | bytes 33685504 | tf_op jit(solution)/shard_map/reduce_window_sum
  80.4 14.7 %copy.12 = f32[1024,32,128]{0,2,1:T(8,128)S(1)} copy(f32[1024,32,128]{0,1,2:T(8,128)S(1)} %broadcast_add_fusion) | data formatting | bytes 33554432 | tf_op jit(solution)/shard_map/reduce_window_sum
  95.2 0.0 copy-start
  95.2 5.7 %copy-done = f32[1024,32,128]{0,2,1:T(8,128)} copy-done((f32[1024,32,128]{0,2,1:T(8,128)}, f32[1024,32,128]{0,2,1:T(8,128)S(1)}, u32[]{:S(2)}) %copy-start) | copy-done | bytes 16777240
  100.9 32.5 %all-gather.1 = f32[32,2,1024]{2,1,0:T(2,128)S(1)} all-gather(f32[1,2,1024]{2,1,0:T(2,128)S(1)} %maximum_bitcast_fusion), channel_id=2, replica_groups=mesh['dp'=1,'vp'=32] {'vp'}, dimensions={0}, use_global_device_ids=true | all-gather | bytes 270336 | tf_op jit(solution)/shard_map/all_gather | solution.py:15
  133.4 0.2 fusion.10
  133.7 0.1 select_reduce_fusion
  133.8 0.0 copy-start.1
  133.8 11.7 %fusion.3 = f32[1024,4008]{0,1:T(8,128)} fusion(f32[1024,4096]{0,1:T(8,128)} %bitcast.36, f32[1024]{0:T(1024)S(1)} %get-tuple-element.3, f32[1024]{0:T(1024)S(1)} %get-tuple-element.2, f32[1024]{0:T(1024)S(1)} %subtract_exponential_fusion.1), kind=kLoop, calls=%fused_computation.5 | loop fusion | flops 12312576 | bytes 32845824 | tf_op jit(solution)/shard_map/div | solution.py:23
  145.5 0.0 copy-done.1
  145.6 45.4 %gather_fusion = f32[1024]{0:T(1024)S(1)} fusion(f32[1024,4008]{0,1:T(8,128)} %fusion.3, s32[1024]{0:T(1024)S(1)} %bitcast.33), kind=kCustom, calls=%fused_computation | custom fusion | bytes 16384 | tf_op jit(solution)/shard_map/jit(take_along_axis)/gather | solution.py:26
  191.0 48.3 %psum.7 = f32[1024]{0:T(1024)} all-reduce(f32[1024]{0:T(1024)S(1)} %select_select_fusion), channel_id=1, replica_groups=mesh['dp'=1,'vp'=32] {'vp'}, use_global_device_ids=true, to_apply=%region_6.7 | all-reduce | flops 1024 | bytes 8192 | tf_op jit(solution)/shard_map/psum | solution.py:27
  (10 shorter events, 0.1 us)
Async XLA Ops:
  0.6 42.8 %copy-start.2 = (f32[1024]{0:T(1024)S(1)}, f32[1024]{0:T(1024)}, u32[]{:S(2)}) copy-start(f32[1024]{0:T(1024)} %param.6) | copy-start | bytes 12292
  95.2 5.7 %copy-start = (f32[1024,32,128]{0,2,1:T(8,128)}, f32[1024,32,128]{0,2,1:T(8,128)S(1)}, u32[]{:S(2)}) copy-start(f32[1024,32,128]{0,2,1:T(8,128)S(1)} %copy.12) | copy-start | bytes 50331652
  133.8 11.7 %copy-start.1 = (s32[1024]{0:T(1024)S(1)}, s32[1024]{0:T(1024)}, u32[]{:S(2)}) copy-start(s32[1024]{0:T(1024)} %param.7) | copy-start | bytes 12292
where the time goes:
time: 240 us; the launch traced here: 239 us
  blocking collectives  80.9 us (34%)
  local copies, waits for them, and re-layouts  74 us (31%)
  matrix products  42.8 us (18%)
  other arithmetic  40.9 us (17%)
    psum x1, blocking collectives, local_fn(): cdf_target = lax.psum(jnp.where(inside, picked, 0.0), 'vp')  48.3 us
    gather x1, local copies, waits for them, and re-layouts, local_fn(): jnp.take_along_axis(cdf_local, jnp.clip(local_pos, 0, shard_width - 1)[:,...  45.4 us
    dot_general x1, matrix products, local_fn(): jnp.dot(h_rows, w_cols, preferred_element_type=jnp.float32)  42.8 us
    all_gather x1, blocking collectives, local_fn(): all_stats = lax.all_gather(pair_stats, 'vp')  32.5 us
    another operation x3, other arithmetic  26.5 us
    another operation x3, local copies, waits for them, and re-layouts  15.7 us
    div x1, other arithmetic, local_fn(): (run_sum * jnp.exp(local_max - glob_max)[:, None] + offset[:, None]) / gl...  11.7 us
    pad x1, local copies, waits for them, and re-layouts  7.18 us

commit v1 on v0

v1 whole, which is shorter than its diff:
```python
import functools
import math
import jax
import jax.numpy as jnp
from jax import lax
from jax.experimental import pallas as pl
from jax.experimental.pallas import tpu as pltpu
from jax.sharding import PartitionSpec as P

LOG2E = math.log2(math.e)
LANES = 128
SUBLANES = 8
CHUNK = 512
SEG = 128
UNIT = 256
FIRST_UNITS = 2


def exp_of(x):
    return jnp.exp2(x * LOG2E)


def spread(row):
    return jnp.broadcast_to(row, (SUBLANES, LANES))


def main_kernel(wt_hbm, h_hbm, tau_ref, tgt_ref, c_ref, stat_ref, mh,
                w_v, h_v, z_v, m_st, s_st, t_st, w_sem, h_sem):
    me = lax.axis_index("vp")
    width, depth = wt_hbm.shape
    rows = h_hbm.shape[0]
    units = rows // UNIT
    groups = UNIT // LANES
    n_chunk = pl.cdiv(width, CHUNK)
    n_seg = mh.shape[0]

    def size_of(s):
        return min(CHUNK, width - s * CHUNK)

    def h_copy(u):
        r = pl.ds(u * UNIT, UNIT)
        return pltpu.make_async_copy(h_hbm.at[r, :], h_v.at[r, :], h_sem.at[u])

    def w_copy(s):
        v = pl.ds(s * CHUNK, size_of(s))
        return pltpu.make_async_copy(wt_hbm.at[v, :], w_v.at[v, :], w_sem.at[s])

    for u in range(FIRST_UNITS):
        h_copy(u).start()
    for s in range(n_chunk):
        w_copy(s).start()
    for u in range(FIRST_UNITS, units):
        h_copy(u).start()

    sub = lax.broadcasted_iota(jnp.int32, (SUBLANES, LANES), 0)

    m_st[...] = jnp.full_like(m_st, -jnp.inf)
    s_st[...] = jnp.zeros_like(s_st)
    t_st[...] = jnp.zeros_like(t_st)

    def prefix(x):
        for step in (1, 2, 4):
            x = x + jnp.where(sub >= step, pltpu.roll(x, step, axis=0), 0.0)
        return x

    def all_sublanes(op, x):
        for step in (4, 2, 1):
            x = op(x, pltpu.roll(x, step, axis=0))
        return x

    def aligned(x):
        return x if isinstance(x, int) else pl.multiple_of(x, LANES)

    def epilogue(r0, nr, s, slot):
        for g in range(nr // LANES):
            rg = r0 // LANES + g
            lanes = pl.ds(aligned(r0 + g * LANES), LANES)
            tau = spread(tau_ref[pl.ds(rg, 1), :])
            tgt = spread(tgt_ref[pl.ds(rg, 1), :]) - me * width
            m = m_st[:, lanes]
            run = s_st[:, lanes]
            tacc = t_st[:, lanes]
            for j in range(pl.cdiv(size_of(s), SEG)):
                v0 = s * CHUNK + j * SEG
                used = min(SEG, width - v0) // SUBLANES
                zt = [z_v[slot, j * SEG + i * SUBLANES:j * SEG + (i + 1) * SUBLANES,
                          g * LANES:(g + 1) * LANES] * tau for i in range(used)]
                bm = zt
                while len(bm) > 1:
                    bm = [jnp.maximum(*bm[i:i + 2]) if i + 1 < len(bm) else bm[i] for i in range(0, len(bm), 2)]
                m_new = jnp.maximum(m, all_sublanes(jnp.maximum, bm[0]))
                alpha = exp_of(m - m_new)
                m = m_new
                run = run * alpha
                tacc = tacc * alpha
                for i in range(used):
                    pre = prefix(exp_of(zt[i] - m))
                    cur = pre + run
                    run = run + spread(pre[SUBLANES - 1:SUBLANES, :])
                    tacc = tacc + jnp.where(sub == tgt - (v0 + i * SUBLANES), cur, 0.0)
                    c_ref[v0 + i * SUBLANES:v0 + (i + 1) * SUBLANES, lanes] = cur
                mh[v0 // SEG:v0 // SEG + 1, lanes] = m[0:1, :]
            m_st[:, lanes] = m
            s_st[:, lanes] = run
            t_st[:, lanes] = tacc

    def pack_stats(u):
        for g in range(groups):
            rg = u * groups + g
            lanes = pl.ds(aligned(rg * LANES), LANES)
            stat_ref[0, pl.ds(rg, 1), :] = m_st[0:1, lanes]
            stat_ref[1, pl.ds(rg, 1), :] = s_st[0:1, lanes]
            stat_ref[2, pl.ds(rg, 1), :] = all_sublanes(jnp.add, t_st[:, lanes])[0:1, :]

    def dot_tile(r0, nr, s, slot, lane0=0):
        c0, size = s * CHUNK, size_of(s)
        z_v[slot, 0:size, lane0:lane0 + nr] = lax.dot_general(
            w_v[c0:c0 + size, :], h_v[pl.ds(r0, nr), :], (((1,), (1,)), ((), ())),
            preferred_element_type=jnp.float32)

    last = n_chunk - 1
    first_rows = FIRST_UNITS * UNIT
    for u in range(FIRST_UNITS):
        h_copy(u).wait()
    for s in range(last):
        w_copy(s).wait()
        if s > 0:
            epilogue(0, first_rows, s - 1, (s - 1) % 2)
        dot_tile(0, first_rows, s, s % 2)
    w_copy(last).wait()
    epilogue(0, first_rows, last - 1, (last - 1) % 2)
    for u in range(FIRST_UNITS):
        if u > 0:
            epilogue((u - 1) * UNIT, UNIT, last, (last + u - 1) % 2)
            pack_stats(u - 1)
        dot_tile(u * UNIT, UNIT, last, (last + u) % 2)
    lag = (last + FIRST_UNITS - 1) % 2

    def unit(u, carry):
        r0 = pl.multiple_of(u * UNIT, UNIT)
        h_copy(u).wait()
        epilogue(r0 - UNIT, UNIT, last, lag)
        pack_stats(u - 1)
        for s in range(n_chunk):
            slot = (lag + 1 + s) % 2
            if s > 0:
                epilogue(r0, UNIT, s - 1, 1 - slot)
            dot_tile(r0, UNIT, s, slot)
        return carry

    lax.fori_loop(FIRST_UNITS, units, unit, 0)
    epilogue((units - 1) * UNIT, UNIT, last, (lag + 1 + last) % 2)
    pack_stats(units - 1)


def exchange_kernel(n, width, stat_ref, mh_ref, tgt_ref, ab_ref, ct_ref, recv_v, send_sem, recv_sem):
    me = lax.axis_index("vp")
    n_seg = mh_ref.shape[0]
    n_rg = tgt_ref.shape[0]
    barrier = pltpu.get_barrier_semaphore()

    def peer(k):
        return {"vp": lax.rem(me + k, n)}

    def greet(k, carry):
        pl.semaphore_signal(barrier, inc=1, device_id=peer(k), device_id_type=pl.DeviceIdType.MESH)
        return carry

    def copy(k):
        return pltpu.make_async_remote_copy(
            src_ref=stat_ref, dst_ref=recv_v.at[k - 1], send_sem=send_sem.at[k - 1], recv_sem=recv_sem.at[k - 1],
            device_id=peer(k), device_id_type=pl.DeviceIdType.MESH)

    def send(k, carry):
        copy(k).start()
        return carry

    def wait_recv(k, carry):
        copy(k).wait_recv()
        return carry

    def wait_send(k, carry):
        copy(k).wait_send()
        return carry

    lax.fori_loop(1, n, greet, 0)
    pl.semaphore_wait(barrier, n - 1)
    lax.fori_loop(1, n, send, 0)
    lax.fori_loop(1, n, wait_recv, 0)

    gm = stat_ref[0]
    for k in range(1, n):
        gm = jnp.maximum(gm, recv_v[k - 1, 0])
    tgt = tgt_ref[...]
    f = exp_of(stat_ref[0] - gm)
    sc = stat_ref[1] * f
    total = sc
    before = jnp.zeros_like(sc)
    hit = stat_ref[2] * f + jnp.where((me + 1) * width <= tgt, sc, 0.0)
    for k in range(1, n):
        f = exp_of(recv_v[k - 1, 0] - gm)
        sc = recv_v[k - 1, 1] * f
        src = lax.rem(me + n - k, n)
        total = total + sc
        before = before + jnp.where(src < me, sc, 0.0)
        hit = hit + recv_v[k - 1, 2] * f + jnp.where((src + 1) * width <= tgt, sc, 0.0)
    ct_ref[...] = hit / total
    off = before / total
    for g in range(n_rg):
        lanes = slice(g * LANES, (g + 1) * LANES)
        ab_ref[0:n_seg, lanes] = exp_of(mh_ref[:, lanes] - gm[g:g + 1, :]) / total[g:g + 1, :]
        ab_ref[n_seg:n_seg + 1, lanes] = off[g:g + 1, :]
    lax.fori_loop(1, n, wait_send, 0)


def table_kernel(c_ref, ab_ref, ct_ref, out_hbm, ct_out, stage, sem):
    width, rows = out_hbm.shape
    ct_out[...] = ct_ref[...]
    n_seg = pl.cdiv(width, SEG)

    def copy(t):
        v = pl.ds(t * SEG, min(SEG, width - t * SEG))
        return pltpu.make_async_copy(stage.at[v, :], out_hbm.at[v, :], sem.at[t])

    for t in range(n_seg):
        v0 = t * SEG
        size = min(SEG, width - v0)
        stage[v0:v0 + size, :] = c_ref[v0:v0 + size, :] * ab_ref[t:t + 1, :] + ab_ref[n_seg:n_seg + 1, :]
        copy(t).start()
    for t in range(n_seg):
        copy(t).wait()


def solution(mesh):
    n = mesh.shape["vp"]

    def local_fn(h_rows, w_cols, tau_rows, tgt_rows):
        rows, depth = h_rows.shape
        width = w_cols.shape[1]
        units = rows // UNIT
        n_rg = rows // LANES
        n_seg = pl.cdiv(width, SEG)
        ab_rows = pl.cdiv(n_seg + 1, SUBLANES) * SUBLANES
        vmem = pl.BlockSpec(memory_space=pltpu.VMEM)
        hbm = pl.BlockSpec(memory_space=pl.ANY)
        tau2, tgt2 = tau_rows.reshape(n_rg, LANES), tgt_rows.reshape(n_rg, LANES)
        c, stat, mh = pl.pallas_call(
            main_kernel,
            name="main_kernel",
            out_shape=(pltpu.VMEM((width, rows), jnp.float32),
                       pltpu.VMEM((3, n_rg, LANES), jnp.float32),
                       pltpu.VMEM((n_seg, rows), jnp.float32)),
            in_specs=[hbm, hbm, vmem, vmem],
            out_specs=(vmem, vmem, vmem),
            scratch_shapes=[
                pltpu.VMEM((width, depth), jnp.bfloat16),
                pltpu.VMEM((rows, depth), jnp.bfloat16),
                pltpu.VMEM((2, CHUNK, FIRST_UNITS * UNIT), jnp.float32),
                pltpu.VMEM((SUBLANES, rows), jnp.float32),
                pltpu.VMEM((SUBLANES, rows), jnp.float32),
                pltpu.VMEM((SUBLANES, rows), jnp.float32),
                pltpu.SemaphoreType.DMA((pl.cdiv(width, CHUNK),)),
                pltpu.SemaphoreType.DMA((units,)),
            ],
            compiler_params=pltpu.CompilerParams(vmem_limit_bytes=45 * 1024 * 1024),
        )(w_cols.T, h_rows, tau2, tgt2)
        stat, mh, c = (pltpu.with_memory_space_constraint(x, pltpu.VMEM) for x in (stat, mh, c))
        ab, ct = pl.pallas_call(
            functools.partial(exchange_kernel, n, width),
            name="exchange_kernel",
            out_shape=(pltpu.VMEM((ab_rows, rows), jnp.float32), pltpu.VMEM((n_rg, LANES), jnp.float32)),
            in_specs=[vmem, vmem, vmem],
            out_specs=(vmem, vmem),
            scratch_shapes=[
                pltpu.VMEM((n - 1, 3, n_rg, LANES), jnp.float32),
                pltpu.SemaphoreType.DMA((n - 1,)),
                pltpu.SemaphoreType.DMA((n - 1,)),
            ],
            compiler_params=pltpu.CompilerParams(
                collective_id=0, has_side_effects=True, vmem_limit_bytes=4 * 1024 * 1024),
        )(stat, mh, tgt2)
        table, ct2 = pl.pallas_call(
            table_kernel,
            name="table_kernel",
            out_shape=(jax.ShapeDtypeStruct((width, rows), jnp.float32),
                       jax.ShapeDtypeStruct((n_rg, LANES), jnp.float32)),
            in_specs=[vmem, vmem, vmem],
            out_specs=(hbm, vmem),
            scratch_shapes=[pltpu.VMEM((width, rows), jnp.float32),
                            pltpu.SemaphoreType.DMA((n_seg,))],
            compiler_params=pltpu.CompilerParams(vmem_limit_bytes=20 * 1024 * 1024),
        )(*(pltpu.with_memory_space_constraint(x, pltpu.VMEM) for x in (c, ab, ct)))
        return table.T, ct2.reshape(rows)

    return jax.shard_map(
        local_fn,
        mesh=mesh,
        in_specs=(P("dp", None), P(None, "vp"), P("dp"), P("dp")),
        out_specs=(P("dp", "vp"), P("dp")),
        check_vma=False,
    )
```

time: 240 us -> 76.5 us (0.32)
  blocking collectives: 80.9 us -> 0 us
  Pallas kernels: 0 us -> 75.5 us
  local copies, waits for them, and re-layouts: 74 us -> 0.01 us
  matrix products: 42.8 us -> 0 us
  other arithmetic: 40.9 us -> 0 us
    pallas_call x0 -> x3, Pallas kernels: none -> 75.5 us  [the longest x1 52.4 us: local_fn(): pl.pallas_call(main_kernel, name='main_kernel', out_shape=(pltpu.VMEM((wi...]
    psum x1 -> x0, blocking collectives: 48.3 us -> none  [local_fn(): cdf_target = lax.psum(jnp.where(inside, picked, 0.0), 'vp')]
    gather x1 -> x0, local copies, waits for them, and re-layouts: 45.4 us -> none  [local_fn(): jnp.take_along_axis(cdf_local, jnp.clip(local_pos, 0, shard_width - 1)[:,...]
    dot_general x1 -> x0, matrix products: 42.8 us -> none  [local_fn(): jnp.dot(h_rows, w_cols, preferred_element_type=jnp.float32)]
    all_gather x1 -> x0, blocking collectives: 32.5 us -> none  [local_fn(): all_stats = lax.all_gather(pair_stats, 'vp')]
    another operation x3 -> x0, other arithmetic: 26.5 us -> none
    another operation x4 -> x0, local copies, waits for them, and re-layouts: 15.7 us -> none
    div x1 -> x0, other arithmetic: 11.7 us -> none  [local_fn(): (run_sum * jnp.exp(local_max - glob_max)[:, None] + offset[:, None]) / gl...]
where the time goes in v1:
time: 76.5 us; the launch traced here: 76.3 us
  Pallas kernels  75.5 us (99%)
  between operations  0.82 us (1%)
    pallas_call x1, Pallas kernels, local_fn(): pl.pallas_call(main_kernel, name='main_kernel', out_shape=(pltpu.VMEM((wi...  52.4 us
    pallas_call x1, Pallas kernels, local_fn(): pl.pallas_call(functools.partial(exchange_kernel, n, width), name='exchan...  16.5 us
    pallas_call x1, Pallas kernels, local_fn(): pl.pallas_call(table_kernel, name='table_kernel', out_shape=(jax.ShapeDty...  6.59 us

profile of v1, /device:TPU:97, one launch (start us, length us, event | category | flops | bytes accessed | tf_op | source)
XLA Modules:
  0.0 76.3 jit_solution(6426983485998047314)
XLA Ops:
  0.6 0.0 copy-start
  0.6 52.4 %main_kernel.1 = (f32[4008,1024]{1,0:T(8,128)S(1)}, f32[3,8,128]{2,1,0:T(8,128)S(1)}, f32[32,1024]{1,0:T(8,128)S(1)}) custom-call(bf16[4008,4096]{1,0:T(8,128)(2,1)} %bitcast.7, bf16[1024,4096]{1,0:T(8,128)(2,1)} %h_hbm.1, f32[8,128]{1,0:T(8,128)} %bitcast.8, s32[8,128]{1,0:T(8,128)} %bitcast.5), custom_call_target="tpu_custom_call" | custom-call | tf_op jit(solution)/shard_map/main_kernel/pallas_call | solution.py:247
  53.0 0.0 copy-done
  53.1 16.5 %exchange_kernel.1 = (f32[40,1024]{1,0:T(8,128)S(1)}, f32[8,128]{1,0:T(8,128)S(1)}) custom-call(f32[3,8,128]{2,1,0:T(8,128)S(1)} %get-tuple-element.10.stat_ref, f32[32,1024]{1,0:T(8,128)S(1)} %get-tuple-element.11.mh_ref, s32[8,128]{1,0:T(8,128)S(1)} %bitcast.6), custom_call_target="tpu_custom_call" | custom-call | tf_op jit(solution)/shard_map/exchange_kernel/pallas_call | solution.py:268
  69.6 6.6 %table_kernel.1 = (f32[4008,1024]{1,0:T(8,128)}, f32[8,128]{1,0:T(8,128)}) custom-call(f32[4008,1024]{1,0:T(8,128)S(1)} %get-tuple-element.9.c_ref, f32[40,1024]{1,0:T(8,128)S(1)} %get-tuple-element.12.ab_ref, f32[8,128]{1,0:T(8,128)S(1)} %get-tuple-element.13.ct_ref), custom_call_target="tpu_custom_call" | custom-call | tf_op jit(solution)/shard_map/table_kernel/pallas_call | solution.py:282
Async XLA Ops:
  0.6 52.4 %copy-start = (s32[1024]{0:T(1024)S(1)}, s32[1024]{0:T(1024)}, u32[]{:S(2)}) copy-start(s32[1024]{0:T(1024)} %param.7) | copy-start | bytes 12292

commit v2 on v1

--- a/solution.py
+++ b/solution.py
@@ -12,6 +12,7 @@
 SUBLANES = 8
 CHUNK = 512
 SEG = 128
+PIECE = 64
 UNIT = 256
 FIRST_UNITS = 2
 
@@ -42,15 +43,33 @@
         return pltpu.make_async_copy(h_hbm.at[r, :], h_v.at[r, :], h_sem.at[u])
 
     def w_copy(s):
-        v = pl.ds(s * CHUNK, size_of(s))
+        v = pl.ds(s * CHUNK, size_of(s) if isinstance(s, int) else CHUNK)
         return pltpu.make_async_copy(wt_hbm.at[v, :], w_v.at[v, :], w_sem.at[s])
 
+    def start(src, dst, sem, r0, nr):
+        def piece(i, carry):
+            r = pl.ds(pl.multiple_of(r0 + i * PIECE, SUBLANES), PIECE)
+            pltpu.make_async_copy(src.at[r, :], dst.at[r, :], sem).start()
+            return carry
+        lax.fori_loop(0, nr // PIECE, piece, 0)
+        rest = nr % PIECE
+        if rest:
+            r = pl.ds(r0 + nr - rest, rest)
+            pltpu.make_async_copy(src.at[r, :], dst.at[r, :], sem).start()
+
+    def start_h(u):
+        start(h_hbm, h_v, h_sem.at[u], u * UNIT, UNIT)
+
+    def start_w(s):
+        start(wt_hbm, w_v, w_sem.at[s], s * CHUNK, size_of(s))
+
     for u in range(FIRST_UNITS):
-        h_copy(u).start()
-    for s in range(n_chunk):
-        w_copy(s).start()
+        start_h(u)
+    start_w(0)
     for u in range(FIRST_UNITS, units):
-        h_copy(u).start()
+        start_h(u)
+    for s in range(1, n_chunk):
+        start_w(s)
 
     sub = lax.broadcasted_iota(jnp.int32, (SUBLANES, LANES), 0)
 
@@ -119,37 +138,62 @@
             preferred_element_type=jnp.float32)
 
     last = n_chunk - 1
-    first_rows = FIRST_UNITS * UNIT
+    half = FIRST_UNITS * UNIT
+    pending = []
+
+    def tile(r0, nr, s):
+        slot = 0
+        if pending:
+            done = pending.pop()
+            slot = 1 - done[3]
+            epilogue(*done)
+        dot_tile(r0, nr, s, slot)
+        pending.append((r0, nr, s, slot))
+
+    def wait_w(s, carry):
+        w_copy(s).wait()
+        return carry
+
+    def wait_h(u, carry):
+        h_copy(u).wait()
+        return carry
+
     for u in range(FIRST_UNITS):
         h_copy(u).wait()
-    for s in range(last):
-        w_copy(s).wait()
-        if s > 0:
-            epilogue(0, first_rows, s - 1, (s - 1) % 2)
-        dot_tile(0, first_rows, s, s % 2)
+    w_copy(0).wait()
+    tile(0, half, 0)
+    w_copy(1).wait()
+    lax.fori_loop(FIRST_UNITS, units, wait_h, 0)
+    tile(half, half, 0)
+    for s in range(1, 2):
+        tile(0, half, s)
+        tile(half, half, s)
+    lax.fori_loop(2, 4, wait_w, 0)
+    for s in range(2, 4):
+        tile(0, half, s)
+        tile(half, half, s)
     w_copy(last).wait()
-    epilogue(0, first_rows, last - 1, (last - 1) % 2)
+    lax.fori_loop(4, last, wait_w, 0)
+    for s in range(4, last):
+        tile(0, half, s)
     for u in range(FIRST_UNITS):
+        tile(u * UNIT, UNIT, last)
         if u > 0:
-            epilogue((u - 1) * UNIT, UNIT, last, (last + u - 1) % 2)
             pack_stats(u - 1)
-        dot_tile(u * UNIT, UNIT, last, (last + u) % 2)
-    lag = (last + FIRST_UNITS - 1) % 2
+    lag = pending.pop()[3]
 
     def unit(u, carry):
         r0 = pl.multiple_of(u * UNIT, UNIT)
-        h_copy(u).wait()
-        epilogue(r0 - UNIT, UNIT, last, lag)
-        pack_stats(u - 1)
-        for s in range(n_chunk):
-            slot = (lag + 1 + s) % 2
-            if s > 0:
-                epilogue(r0, UNIT, s - 1, 1 - slot)
-            dot_tile(r0, UNIT, s, slot)
+        pending.append((r0 - UNIT, UNIT, last, lag))
+        for s in range(4, n_chunk):
+            tile(r0, UNIT, s)
+            if s == 4:
+                pack_stats(u - 1)
+        pending.pop()
         return carry
 
     lax.fori_loop(FIRST_UNITS, units, unit, 0)
-    epilogue((units - 1) * UNIT, UNIT, last, (lag + 1 + last) % 2)
+    epilogue((units - 1) * UNIT, UNIT, last, lag)
     pack_stats(units - 1)
 
 

time: 76.5 us -> 68.4 us (0.89)
  Pallas kernels: 75.5 us -> 67.5 us
    pallas_call x1, Pallas kernels: 52.4 us -> 44.4 us  [local_fn(): pl.pallas_call(main_kernel, name='main_kernel', out_shape=(pltpu.VMEM((wi...]
where the time goes in v2:
time: 68.4 us; the launch traced here: 68.3 us
  Pallas kernels  67.5 us (99%)
  between operations  0.84 us (1%)
    pallas_call x1, Pallas kernels, local_fn(): pl.pallas_call(main_kernel, name='main_kernel', out_shape=(pltpu.VMEM((wi...  44.4 us
    pallas_call x1, Pallas kernels, local_fn(): pl.pallas_call(functools.partial(exchange_kernel, n, width), name='exchan...  16.5 us
    pallas_call x1, Pallas kernels, local_fn(): pl.pallas_call(table_kernel, name='table_kernel', out_shape=(jax.ShapeDty...  6.59 us

profile of v2, /device:TPU:97, one launch (start us, length us, event | category | flops | bytes accessed | tf_op | source)
XLA Modules:
  0.0 68.3 jit_solution(14980204832524559302)
XLA Ops:
  0.6 0.0 copy-start
  0.6 44.4 %main_kernel.1 = (f32[4008,1024]{1,0:T(8,128)S(1)}, f32[3,8,128]{2,1,0:T(8,128)S(1)}, f32[32,1024]{1,0:T(8,128)S(1)}) custom-call(bf16[4008,4096]{1,0:T(8,128)(2,1)} %bitcast.7, bf16[1024,4096]{1,0:T(8,128)(2,1)} %h_hbm.1, f32[8,128]{1,0:T(8,128)} %bitcast.8, s32[8,128]{1,0:T(8,128)} %bitcast.5), custom_call_target="tpu_custom_call" | custom-call | tf_op jit(solution)/shard_map/main_kernel/pallas_call | solution.py:291
  45.0 0.0 copy-done
  45.0 16.5 %exchange_kernel.1 = (f32[40,1024]{1,0:T(8,128)S(1)}, f32[8,128]{1,0:T(8,128)S(1)}) custom-call(f32[3,8,128]{2,1,0:T(8,128)S(1)} %get-tuple-element.10.stat_ref, f32[32,1024]{1,0:T(8,128)S(1)} %get-tuple-element.11.mh_ref, s32[8,128]{1,0:T(8,128)S(1)} %bitcast.6), custom_call_target="tpu_custom_call" | custom-call | tf_op jit(solution)/shard_map/exchange_kernel/pallas_call | solution.py:312
  61.5 6.6 %table_kernel.1 = (f32[4008,1024]{1,0:T(8,128)}, f32[8,128]{1,0:T(8,128)}) custom-call(f32[4008,1024]{1,0:T(8,128)S(1)} %get-tuple-element.9.c_ref, f32[40,1024]{1,0:T(8,128)S(1)} %get-tuple-element.12.ab_ref, f32[8,128]{1,0:T(8,128)S(1)} %get-tuple-element.13.ct_ref), custom_call_target="tpu_custom_call" | custom-call | tf_op jit(solution)/shard_map/table_kernel/pallas_call | solution.py:326
Async XLA Ops:
  0.6 44.4 %copy-start = (s32[1024]{0:T(1024)S(1)}, s32[1024]{0:T(1024)}, u32[]{:S(2)}) copy-start(s32[1024]{0:T(1024)} %param.7) | copy-start | bytes 12292

commit v3 on v2

v3 whole, which is shorter than its diff:
```python
import functools
import math
import jax
import jax.numpy as jnp
from jax import lax
from jax.experimental import pallas as pl
from jax.experimental.pallas import tpu as pltpu
from jax.sharding import PartitionSpec as P

LOG2E = math.log2(math.e)
LANES = 128
SUBLANES = 8
CHUNK = 512
SEG = 128
UNIT = 256
PIECE = 64
HEAD_CHUNKS = 6


def exp_of(x):
    return jnp.exp2(x * LOG2E)


def spread(row):
    return jnp.broadcast_to(row, (SUBLANES, LANES))


def all_sublanes(op, x):
    for step in (4, 2, 1):
        x = op(x, pltpu.roll(x, step, axis=0))
    return x


def prefix8(x, sub, axis):
    for step in (1, 2, 4):
        x = x + jnp.where(sub >= step, pltpu.roll(x, step, axis=axis), 0.0)
    return x


def main_kernel(wt_hbm, h_hbm, tau_ref, tgt_ref, c_ref, stat_ref, st_ref, mh,
                w_v, w_t, h_lo, h_hi, z_v, m_st, s_st, t_st, w_sem, h_sem):
    me = lax.axis_index("vp")
    width, depth = wt_hbm.shape
    rows = h_hbm.shape[0]
    half = rows // 2
    units = rows // UNIT
    groups = UNIT // LANES
    n_chunk = pl.cdiv(width, CHUNK)
    last = n_chunk - 1
    head = HEAD_CHUNKS * CHUNK

    def size_of(s):
        return min(CHUNK, width - s * CHUNK)

    def start(src, s0, dst, d0, sem, nr):
        def piece(i, carry):
            off = pl.multiple_of(i * PIECE, PIECE)
            pltpu.make_async_copy(src.at[pl.ds(s0 + off, PIECE), :], dst.at[pl.ds(d0 + off, PIECE), :], sem).start()
            return carry
        lax.fori_loop(0, nr // PIECE, piece, 0)
        rest = nr % PIECE
        if rest:
            off = nr - rest
            pltpu.make_async_copy(src.at[pl.ds(s0 + off, rest), :], dst.at[pl.ds(d0 + off, rest), :], sem).start()

    def w_at(s):
        return (w_v, s * CHUNK) if s < HEAD_CHUNKS else (w_t, s * CHUNK - head)

    def h_at(r0):
        return (h_lo, r0) if r0 < half else (h_hi, r0 - half)

    def start_h(k):
        start(h_hbm, k * half, *h_at(k * half), h_sem.at[k], half)

    def wait_h(k):
        dst, _ = h_at(k * half)
        pltpu.make_async_copy(h_hbm.at[pl.ds(k * half, half), :], dst, h_sem.at[k]).wait()

    def start_w(s):
        start(wt_hbm, s * CHUNK, *w_at(s), w_sem.at[s], size_of(s))

    def wait_w(s):
        dst, d0 = w_at(s)
        pltpu.make_async_copy(wt_hbm.at[pl.ds(s * CHUNK, size_of(s)), :],
                              dst.at[pl.ds(d0, size_of(s)), :], w_sem.at[s]).wait()

    start_h(0)
    start_w(0)
    start_h(1)
    for s in range(1, n_chunk):
        start_w(s)

    sub = lax.broadcasted_iota(jnp.int32, (SUBLANES, LANES), 0)

    m_st[...] = jnp.full_like(m_st, -jnp.inf)
    s_st[...] = jnp.zeros_like(s_st)
    t_st[...] = jnp.zeros_like(t_st)

    def epilogue(r0, nr, s, slot):
        for g in range(nr // LANES):
            rg = r0 // LANES + g
            lanes = slice(r0 + g * LANES, r0 + (g + 1) * LANES)
            tau = spread(tau_ref[rg:rg + 1, :])
            tgt = spread(tgt_ref[rg:rg + 1, :]) - me * width
            m = m_st[:, lanes]
            run = s_st[:, lanes]
            tacc = t_st[:, lanes]
            for j in range(pl.cdiv(size_of(s), SEG)):
                v0 = s * CHUNK + j * SEG
                used = min(SEG, width - v0) // SUBLANES
                zt = [z_v[slot, j * SEG + i * SUBLANES:j * SEG + (i + 1) * SUBLANES,
                          g * LANES:(g + 1) * LANES] * tau for i in range(used)]
                bm = zt
                while len(bm) > 1:
                    bm = [jnp.maximum(*bm[i:i + 2]) if i + 1 < len(bm) else bm[i] for i in range(0, len(bm), 2)]
                m_new = jnp.maximum(m, all_sublanes(jnp.maximum, bm[0]))
                alpha = exp_of(m - m_new)
                m = m_new
                run = run * alpha
                tacc = tacc * alpha
                for i in range(used):
                    pre = prefix8(exp_of(zt[i] - m), sub, 0)
                    cur = pre + run
                    run = run + spread(pre[SUBLANES - 1:SUBLANES, :])
                    tacc = tacc + jnp.where(sub == tgt - (v0 + i * SUBLANES), cur, 0.0)
                    c_ref[v0 + i * SUBLANES:v0 + (i + 1) * SUBLANES, lanes] = cur
                mh[v0 // SEG:v0 // SEG + 1, lanes] = m[0:1, :]
            m_st[:, lanes] = m
            s_st[:, lanes] = run
            t_st[:, lanes] = tacc

    def dot_tile(r0, nr, s, slot):
        w, c0 = w_at(s)
        h, h0 = h_at(r0)
        z_v[slot, 0:size_of(s), 0:nr] = lax.dot_general(
            w[c0:c0 + size_of(s), :], h[h0:h0 + nr, :], (((1,), (1,)), ((), ())),
            preferred_element_type=jnp.float32)

    pending = []

    def tile(r0, nr, s):
        slot = 0
        if pending:
            done = pending.pop()
            slot = 1 - done[3]
            epilogue(*done)
        dot_tile(r0, nr, s, slot)
        pending.append((r0, nr, s, slot))

    def half_wait(k, carry):
        pltpu.make_async_copy(h_hbm.at[pl.ds(0, half // 2), :], h_hi.at[pl.ds(0, half // 2), :], h_sem.at[1]).wait()
        return carry

    def head_wait(s, carry):
        v = pl.ds(s * CHUNK, CHUNK)
        pltpu.make_async_copy(wt_hbm.at[v, :], w_v.at[v, :], w_sem.at[s]).wait()
        return carry

    def tail_wait(i, carry):
        v = pl.ds(0, CHUNK // 2)
        pltpu.make_async_copy(wt_hbm.at[v, :], w_t.at[v, :], w_sem.at[HEAD_CHUNKS + i // 2]).wait()
        return carry

    wait_h(0)
    wait_w(0)
    tile(0, half, 0)
    wait_w(1)
    lax.fori_loop(0, 2, half_wait, 0)
    tile(half, half, 0)
    tile(0, half, 1)
    tile(half, half, 1)
    lax.fori_loop(2, HEAD_CHUNKS, head_wait, 0)
    for s in range(2, HEAD_CHUNKS):
        tile(0, half, s)
        tile(half, half, s)
    wait_w(last)
    lax.fori_loop(0, 2 * (last - HEAD_CHUNKS), tail_wait, 0)
    for s in range(HEAD_CHUNKS, last):
        tile(0, half, s)
    tile(0, UNIT, last)
    tile(UNIT, UNIT, last)
    for s in range(HEAD_CHUNKS, n_chunk):
        tile(half, UNIT, s)
    epilogue(*pending.pop())

    done = (units - 1) * groups
    for rg in range(done):
        lanes = slice(rg * LANES, (rg + 1) * LANES)
        stat_ref[rg:rg + 1, :] = m_st[0:1, lanes]
        stat_ref[done + rg:done + rg + 1, :] = s_st[0:1, lanes]
        stat_ref[2 * done + rg:2 * done + rg + 1, :] = all_sublanes(jnp.add, t_st[:, lanes])[0:1, :]
    rest = slice(done * LANES, rows)
    st_ref[0] = m_st[:, rest]
    st_ref[1] = s_st[:, rest]
    st_ref[2] = t_st[:, rest]


def tail_kernel(n, width, wt_hbm, h_hbm, tau_ref, tgt_ref, stat_ref, st_ref, mh_ref, c_ref, ab_ref, ct_ref,
                w_t, h_t, w_sem, h_sem, z_v, st_v, mh_v, late_v, recv_a, recv_b, send_a, got_a, send_b, got_b):
    me = lax.axis_index("vp")
    n_rg = tgt_ref.shape[0]
    groups = UNIT // LANES
    done = n_rg - groups
    n_seg = mh_ref.shape[0]
    head_seg = HEAD_CHUNKS * CHUNK // SEG
    n_early = recv_a.shape[1]
    n_mixed = 3 * done - n_early
    tail_rows = w_t.shape[0]
    n_tail = pl.cdiv(tail_rows, CHUNK)
    barrier = pltpu.get_barrier_semaphore()

    def peer(k):
        return {"vp": lax.rem(me + k, n)}

    def greet(k, carry):
        pl.semaphore_signal(barrier, inc=1, device_id=peer(k), device_id_type=pl.DeviceIdType.MESH)
        return carry

    def early_copy(k):
        return pltpu.make_async_remote_copy(
            src_ref=stat_ref.at[pl.ds(0, n_early), :], dst_ref=recv_a.at[k - 1],
            send_sem=send_a.at[k - 1], recv_sem=got_a.at[k - 1],
            device_id=peer(k), device_id_type=pl.DeviceIdType.MESH)

    def late_copy(k):
        return pltpu.make_async_remote_copy(
            src_ref=late_v, dst_ref=recv_b.at[k - 1],
            send_sem=send_b.at[k - 1], recv_sem=got_b.at[k - 1],
            device_id=peer(k), device_id_type=pl.DeviceIdType.MESH)

    def each(f):
        def body(k, carry):
            f(k)
            return carry
        lax.fori_loop(1, n, body, 0)

    def size_of(s):
        return min(CHUNK, tail_rows - s * CHUNK)

    def start(src, s0, dst, d0, sem, nr):
        def piece(i, carry):
            off = pl.multiple_of(i * PIECE, PIECE)
            pltpu.make_async_copy(src.at[pl.ds(s0 + off, PIECE), :], dst.at[pl.ds(d0 + off, PIECE), :], sem).start()
            return carry
        lax.fori_loop(0, nr // PIECE, piece, 0)
        rest = nr % PIECE
        if rest:
            off = nr - rest
            pltpu.make_async_copy(src.at[pl.ds(s0 + off, rest), :], dst.at[pl.ds(d0 + off, rest), :], sem).start()

    def start_all():
        start(h_hbm, done * LANES, h_t, 0, h_sem, UNIT)
        for s in range(n_tail):
            start(wt_hbm, HEAD_CHUNKS * CHUNK + s * CHUNK, w_t, s * CHUNK, w_sem.at[s], size_of(s))

    def wait_h():
        pltpu.make_async_copy(h_hbm.at[pl.ds(done * LANES, UNIT), :], h_t, h_sem).wait()

    def wait_w(s):
        v = pl.ds(s * CHUNK, size_of(s))
        pltpu.make_async_copy(wt_hbm.at[pl.ds(HEAD_CHUNKS * CHUNK + s * CHUNK, size_of(s)), :],
                              w_t.at[v, :], w_sem.at[s]).wait()

    def dot_tile(s):
        z_v[s % 2, 0:size_of(s), :] = lax.dot_general(
            w_t[s * CHUNK:s * CHUNK + size_of(s), :], h_t[...], (((1,), (1,)), ((), ())),
            preferred_element_type=jnp.float32)

    def epilogue(s):
        for g in range(groups):
            rg = done + g
            lanes = slice(g * LANES, (g + 1) * LANES)
            tau = tau_ref[rg:rg + 1, :]
            tgt = tgt_ref[rg:rg + 1, :] - (me * width + HEAD_CHUNKS * CHUNK)
            m = st_v[0, :, lanes]
            run = st_v[1, :, lanes]
            tacc = st_v[2, :, lanes]
            for j in range(pl.cdiv(size_of(s), SEG)):
                v0 = s * CHUNK + j * SEG
                size = min(SEG, tail_rows - v0)
                regs = size // SUBLANES
                z = (z_v[s % 2, j * SEG:j * SEG + size, lanes] * tau).reshape(regs, SUBLANES, LANES)
                m_new = jnp.maximum(m, all_sublanes(jnp.maximum, jnp.max(z, axis=0)))
                alpha = exp_of(m - m_new)
                m = m_new
                sub = lax.broadcasted_iota(jnp.int32, (regs, SUBLANES, LANES), 1)
                pre = prefix8(exp_of(z - m[None]), sub, 1)
                ends = jnp.broadcast_to(pre[:, SUBLANES - 1:SUBLANES, :], pre.shape)
                step = 1
                while step < regs:
                    ends = ends + jnp.concatenate([jnp.zeros((step, SUBLANES, LANES), jnp.float32), ends[:-step]])
                    step *= 2
                prior = jnp.concatenate([jnp.zeros((1, SUBLANES, LANES), jnp.float32), ends[:-1]])
                cur = pre + (prior + (run * alpha)[None])
                run = spread(cur[regs - 1, SUBLANES - 1:SUBLANES, :])
                cur = cur.reshape(size, LANES)
                voc = lax.broadcasted_iota(jnp.int32, (size, LANES), 0) + v0
                hit = jnp.where(voc == tgt, cur, 0.0).reshape(regs, SUBLANES, LANES)
                tacc = tacc * alpha + jnp.sum(hit, axis=0)
                c_ref[v0:v0 + size, lanes] = cur
                mh_v[v0 // SEG:v0 // SEG + 1, lanes] = m[0:1, :]
            st_v[0, :, lanes] = m
            st_v[1, :, lanes] = run
            st_v[2, :, lanes] = tacc

    def before(k):
        return lax.rem(me + n - k, n)

    def combine(tgt, m_own, s_own, t_own, m_of, s_of, t_of):
        gm = m_own
        for k in range(1, n):
            gm = jnp.maximum(gm, m_of(k))
        f = exp_of(m_own - gm)
        sc = s_own * f
        total, prev = sc, jnp.zeros_like(sc)
        hit = jnp.where((me + 1) * width <= tgt, sc, 0.0)
        scales = [f]
        for k in range(1, n):
            f = exp_of(m_of(k) - gm)
            sc = s_of(k) * f
            src = before(k)
            total = total + sc
            prev = prev + jnp.where(src < me, sc, 0.0)
            hit = hit + jnp.where((src + 1) * width <= tgt, sc, 0.0)
            scales.append(f)
        return gm, total, prev, hit, scales

    def put_ab(rg, part, gm, total, prev):
        lanes = slice(rg * LANES, (rg + 1) * LANES)
        ab_ref[n_seg:n_seg + 1, lanes] = prev / total
        for r0, seg in part:
            ab_ref[r0:r0 + seg.shape[0], lanes] = exp_of(seg - gm) / total

    each(lambda k: greet(k, 0))
    start_all()
    st_v[...] = st_ref[...]
    wait_h()
    wait_w(0)
    pl.semaphore_wait(barrier, n - 1)
    each(lambda k: early_copy(k).start())
    dot_tile(0)
    for s in range(1, n_tail):
        wait_w(s)
    for s in range(1, n_tail):
        epilogue(s - 1)
        dot_tile(s)
    epilogue(n_tail - 1)
    late_v[0:n_mixed, :] = stat_ref[n_early:n_early + n_mixed, :]
    for g in range(groups):
        lanes = slice(g * LANES, (g + 1) * LANES)
        late_v[n_mixed + g:n_mixed + g + 1, :] = st_v[0, 0:1, lanes]
        late_v[n_mixed + groups + g:n_mixed + groups + g + 1, :] = st_v[1, 0:1, lanes]
        late_v[n_mixed + 2 * groups + g:n_mixed + 2 * groups + g + 1, :] = (
            all_sublanes(jnp.add, st_v[2, :, lanes])[0:1, :])
    each(lambda k: late_copy(k).start())

    each(lambda k: early_copy(k).wait_recv())
    tgt_a = tgt_ref[0:done, :]
    gm, total, prev, hit, scales = combine(
        tgt_a, stat_ref[0:done, :], stat_ref[done:2 * done, :], None,
        lambda k: recv_a[k - 1, 0:done, :], lambda k: recv_a[k - 1, done:2 * done, :], None)
    n_t = done - n_mixed
    hit_a = hit[0:n_t] + stat_ref[2 * done:2 * done + n_t, :] * scales[0][0:n_t]
    for k in range(1, n):
        hit_a = hit_a + recv_a[k - 1, 2 * done:2 * done + n_t, :] * scales[k][0:n_t]
    ct_ref[0:n_t, :] = hit_a / total[0:n_t]
    for rg in range(done):
        put_ab(rg, [(0, mh_ref[:, rg * LANES:(rg + 1) * LANES])],
               gm[rg:rg + 1], total[rg:rg + 1], prev[rg:rg + 1])

    each(lambda k: late_copy(k).wait_recv())
    hit_b = hit[n_t:] + late_v[0:n_mixed, :] * scales[0][n_t:]
    for k in range(1, n):
        hit_b = hit_b + recv_b[k - 1, 0:n_mixed, :] * scales[k][n_t:]
    ct_ref[n_t:done, :] = hit_b / total[n_t:]

    q = [n_mixed + i * groups for i in range(4)]
    gm, total, prev, hit, scales = combine(
        tgt_ref[done:, :], late_v[q[0]:q[1], :], late_v[q[1]:q[2], :], None,
        lambda k: recv_b[k - 1, q[0]:q[1], :], lambda k: recv_b[k - 1, q[1]:q[2], :], None)
    hit = hit + late_v[q[2]:q[3], :] * scales[0]
    for k in range(1, n):
        hit = hit + recv_b[k - 1, q[2]:q[3], :] * scales[k]
    ct_ref[done:, :] = hit / total
    for g in range(groups):
        rg = done + g
        put_ab(rg, [(0, mh_ref[0:head_seg, rg * LANES:(rg + 1) * LANES]),
                    (head_seg, mh_v[:, g * LANES:(g + 1) * LANES])],
               gm[g:g + 1], total[g:g + 1], prev[g:g + 1])
    each(lambda k: early_copy(k).wait_send())
    each(lambda k: late_copy(k).wait_send())


def table_kernel(c_ref, c2_ref, ab_ref, ct_ref, out_hbm, ct_out, stage, sem):
    width, rows = out_hbm.shape
    ct_out[...] = ct_ref[...]
    n_seg = pl.cdiv(width, SEG)
    head = HEAD_CHUNKS * CHUNK

    def copy(t):
        v = pl.ds(t * SEG, min(SEG, width - t * SEG))
        return pltpu.make_async_copy(stage.at[v, :], out_hbm.at[v, :], sem.at[t])

    for t in range(n_seg):
        v0 = t * SEG
        size = min(SEG, width - v0)
        split = rows if v0 < head else rows - UNIT
        lo, hi = slice(0, split), slice(split, rows)
        stage[v0:v0 + size, lo] = c_ref[v0:v0 + size, lo] * ab_ref[t:t + 1, lo] + ab_ref[n_seg:n_seg + 1, lo]
        if split < rows:
            stage[v0:v0 + size, hi] = (c2_ref[v0 - head:v0 - head + size, :] * ab_ref[t:t + 1, hi]
                                       + ab_ref[n_seg:n_seg + 1, hi])
        copy(t).start()
    for t in range(n_seg):
        copy(t).wait()


def solution(mesh):
    n = mesh.shape["vp"]

    def local_fn(h_rows, w_cols, tau_rows, tgt_rows):
        rows, depth = h_rows.shape
        width = w_cols.shape[1]
        n_rg = rows // LANES
        n_seg = pl.cdiv(width, SEG)
        ab_rows = pl.cdiv(n_seg + 1, SUBLANES) * SUBLANES
        vmem = pl.BlockSpec(memory_space=pltpu.VMEM)
        hbm = pl.BlockSpec(memory_space=pl.ANY)
        tau2, tgt2 = tau_rows.reshape(n_rg, LANES), tgt_rows.reshape(n_rg, LANES)
        half = rows // 2
        head = HEAD_CHUNKS * CHUNK
        tail = width - head
        done = n_rg - UNIT // LANES
        n_early = 3 * done // SUBLANES * SUBLANES
        n_late = 3 * n_rg - n_early
        f32 = jnp.float32
        wt = w_cols.T
        c, stat, st, mh = pl.pallas_call(
            main_kernel,
            name="main_kernel",
            out_shape=(pltpu.VMEM((width, rows), f32),
                       pltpu.VMEM((3 * n_rg, LANES), f32),
                       pltpu.VMEM((3, SUBLANES, UNIT), f32),
                       pltpu.VMEM((n_seg, rows), f32)),
            in_specs=[hbm, hbm, vmem, vmem],
            out_specs=(vmem,) * 4,
            scratch_shapes=[
                pltpu.VMEM((head, depth), jnp.bfloat16),
                pltpu.VMEM((tail, depth), jnp.bfloat16),
                pltpu.VMEM((half, depth), jnp.bfloat16),
                pltpu.VMEM((half, depth), jnp.bfloat16),
                pltpu.VMEM((2, CHUNK, half), f32),
                pltpu.VMEM((SUBLANES, rows), f32),
                pltpu.VMEM((SUBLANES, rows), f32),
                pltpu.VMEM((SUBLANES, rows), f32),
                pltpu.SemaphoreType.DMA((pl.cdiv(width, CHUNK),)),
                pltpu.SemaphoreType.DMA((2,)),
            ],
            compiler_params=pltpu.CompilerParams(vmem_limit_bytes=45 * 1024 * 1024),
        )(wt, h_rows, tau2, tgt2)
        in_vmem = lambda *xs: [pltpu.with_memory_space_constraint(x, pltpu.VMEM) for x in xs]
        c, stat, st, mh = in_vmem(c, stat, st, mh)
        c2, ab, ct = pl.pallas_call(
            functools.partial(tail_kernel, n, width),
            name="tail_kernel",
            out_shape=(pltpu.VMEM((tail, UNIT), f32),
                       pltpu.VMEM((ab_rows, rows), f32),
                       pltpu.VMEM((n_rg, LANES), f32)),
            in_specs=[hbm, hbm] + [vmem] * 5,
            out_specs=(vmem,) * 3,
            scratch_shapes=[
                pltpu.VMEM((tail, depth), jnp.bfloat16),
                pltpu.VMEM((UNIT, depth), jnp.bfloat16),
                pltpu.SemaphoreType.DMA((pl.cdiv(tail, CHUNK),)),
                pltpu.SemaphoreType.DMA,
                pltpu.VMEM((2, CHUNK, UNIT), f32),
                pltpu.VMEM((3, SUBLANES, UNIT), f32),
                pltpu.VMEM((pl.cdiv(tail, SEG), UNIT), f32),
                pltpu.VMEM((n_late, LANES), f32),
                pltpu.VMEM((n - 1, n_early, LANES), f32),
                pltpu.VMEM((n - 1, n_late, LANES), f32),
            ] + [pltpu.SemaphoreType.DMA((n - 1,))] * 4,
            compiler_params=pltpu.CompilerParams(
                collective_id=0, has_side_effects=True, vmem_limit_bytes=20 * 1024 * 1024),
        )(*(pltpu.with_memory_space_constraint(x, pltpu.HBM) for x in (wt, h_rows)), tau2, tgt2, stat, st, mh)
        table, ct2 = pl.pallas_call(
            table_kernel,
            name="table_kernel",
            out_shape=(jax.ShapeDtypeStruct((width, rows), jnp.float32),
                       jax.ShapeDtypeStruct((n_rg, LANES), jnp.float32)),
            in_specs=[vmem] * 4,
            out_specs=(hbm, vmem),
            scratch_shapes=[pltpu.VMEM((width, rows), jnp.float32),
                            pltpu.SemaphoreType.DMA((n_seg,))],
            compiler_params=pltpu.CompilerParams(vmem_limit_bytes=20 * 1024 * 1024),
        )(c, *in_vmem(c2, ab, ct))
        return table.T, ct2.reshape(rows)

    return jax.shard_map(
        local_fn,
        mesh=mesh,
        in_specs=(P("dp", None), P(None, "vp"), P("dp"), P("dp")),
        out_specs=(P("dp", "vp"), P("dp")),
        check_vma=False,
    )
```

time: 68.4 us -> 69.8 us (1.020)
  Pallas kernels: 67.5 us -> 68.8 us
    pallas_call x1, Pallas kernels: 16.5 us -> 20.7 us  [local_fn(): pl.pallas_call(functools.partial(tail_kernel, n, width), name='tail_kerne...]
    pallas_call x1, Pallas kernels: 44.4 us -> 41.5 us  [local_fn(): pl.pallas_call(main_kernel, name='main_kernel', out_shape=(pltpu.VMEM((wi...]
where the time goes in v3:
time: 69.8 us; the launch traced here: 69.7 us
  Pallas kernels  68.8 us (99%)
  between operations  0.86 us (1%)
    pallas_call x1, Pallas kernels, local_fn(): pl.pallas_call(main_kernel, name='main_kernel', out_shape=(pltpu.VMEM((wi...  41.5 us
    pallas_call x1, Pallas kernels, local_fn(): pl.pallas_call(functools.partial(tail_kernel, n, width), name='tail_kerne...  20.7 us
    pallas_call x1, Pallas kernels, local_fn(): pl.pallas_call(table_kernel, name='table_kernel', out_shape=(jax.ShapeDty...  6.59 us

profile of v3, /device:TPU:97, one launch (start us, length us, event | category | flops | bytes accessed | tf_op | source)
XLA Modules:
  0.0 69.7 jit_solution(17513523490407667889)
XLA Ops:
  0.6 0.0 copy-start
  0.6 0.0 copy-start.1
  0.6 41.5 %main_kernel.1 = (f32[4008,1024]{1,0:T(8,128)S(1)}, f32[24,128]{1,0:T(8,128)S(1)}, f32[3,8,256]{2,1,0:T(8,128)S(1)}, f32[32,1024]{1,0:T(8,128)S(1)}) custom-call(bf16[4008,4096]{1,0:T(8,128)(2,1)} %bitcast.9, bf16[1024,4096]{1,0:T(8,128)(2,1)} %h_hbm.3, f32[8,128]{1,0:T(8,128)} %bitcast.5, s32[8,128]{1,0:T(8,128)} %bitcast.7), custom_call_target="tpu_custom_call" | custom-call | tf_op jit(solution)/shard_map/main_kernel/pallas_call | solution.py:438
  42.2 0.0 copy-done
  42.2 0.0 copy-done.1
  42.2 20.7 %tail_kernel.1 = (f32[936,256]{1,0:T(8,128)S(1)}, f32[40,1024]{1,0:T(8,128)S(1)}, f32[8,128]{1,0:T(8,128)S(1)}) custom-call(bf16[4008,4096]{1,0:T(8,128)(2,1)} %bitcast.10, bf16[1024,4096]{1,0:T(8,128)(2,1)} %h_hbm.3, f32[8,128]{1,0:T(8,128)S(1)} %bitcast.6, s32[8,128]{1,0:T(8,128)S(1)} %bitcast.8, f32[24,128]{1,0:T(8,128)S(1)} %get-tuple-element.12.stat_ref, ...), custom_call_target="tpu_custom_call" | custom-call | tf_op jit(solution)/shard_map/tail_kernel/pallas_call | solution.py:463
  62.9 6.6 %table_kernel.1 = (f32[4008,1024]{1,0:T(8,128)}, f32[8,128]{1,0:T(8,128)}) custom-call(f32[4008,1024]{1,0:T(8,128)S(1)} %get-tuple-element.11.c_ref, f32[936,256]{1,0:T(8,128)S(1)} %get-tuple-element.15.c2_ref, f32[40,1024]{1,0:T(8,128)S(1)} %get-tuple-element.16.ab_ref, f32[8,128]{1,0:T(8,128)S(1)} %get-tuple-element.17.ct_ref), custom_call_target="tpu_custom_call" | custom-call | tf_op jit(solution)/shard_map/table_kernel/pallas_call | solution.py:486
Async XLA Ops:
  0.6 41.5 %copy-start = (f32[1024]{0:T(1024)S(1)}, f32[1024]{0:T(1024)}, u32[]{:S(2)}) copy-start(f32[1024]{0:T(1024)} %param.6) | copy-start | bytes 12292
  0.6 41.5 %copy-start.1 = (s32[1024]{0:T(1024)S(1)}, s32[1024]{0:T(1024)}, u32[]{:S(2)}) copy-start(s32[1024]{0:T(1024)} %param.7) | copy-start | bytes 12292
